TPU v7x, 256 devices: a whole 4x4x8 slice. The times are simulated.
256 devices in a mesh: feat: 64 (over z, y, x_hi), row: 2 (over x_lo), col: 2 (over core).
Axes of the slice: x: 4 (x_hi: 2, x_lo: 2; x = x_hi * 2 + x_lo), y: 4, z: 8, core: 2. Of those that a mesh axis runs over, the one named last changes fastest.
Arguments:
- local_x: float32 [4, 256, 256], P(('row', 'col'), 'feat'), may hold values from -4 to 4
- dual_var: float32 [4, 256, 256], P(('row', 'col'), 'feat'), may hold values from -2 to 2
- consensus_old: float32 [256, 256], P('feat'), may hold values from -4 to 4
- blocks_data: bfloat16 [4, 256, 512, 256], P(('row', 'col'), 'feat'), may hold values from -0.375 to 0.375
- row_index: int32 [4, 256, 512], P(('row', 'col'), 'feat'), may hold values from 0 to 16383, as said below
- labels: int32 [4, 16384], P(('row', 'col')), may hold values 0 or 1
Outputs:
- solved_x: float32 [4, 256, 256], P(('row', 'col'), 'feat')
- dual_new: float32 [4, 256, 256], P(('row', 'col'), 'feat')
- consensus: float32 [256, 256], P('feat')
- norms: float32 [2], replicated
Inputs may be any that keep to these rules, and one draw needn't show every extreme that they name: `row_index`: the 512 rows of one block are distinct samples of its shard; a sample may appear in no block or in several.
All inputs are finite; a program needn't handle non-finite values. No bound on the sum of `labels` on one device may be relied on, other than what follows from the above.
Results may differ from a plain program's by a relative error of at most 0.0019.
Values sent between devices are 32-bit elements; how exact they have to be, the bound alone decides.
No kernel may reach another device: no remote copies, remote signals or barrier semaphores. Data moves between devices by JAX's collectives and lax.ppermute only.
A program may use at most 64 MiB of HBM per device.

v0:
```python
import jax
import jax.numpy as jnp
from jax import lax
from jax.sharding import Mesh
from jax.sharding import PartitionSpec as P

NEWTON_STEPS = 2
CG_STEPS = 3
FEAT = ("feat_0", "feat_1", "feat_2")
FEAT_ROW_COL = ("feat_0", "feat_1", "feat_2", "row", "col")
penalty = 1.0
damping = 0.5
threshold = 0.05


def filled_up(lines, size):
    spare = -len(lines) % size
    return jnp.pad(lines, [(0, spare)] + [(0, 0)] * (lines.ndim - 1))


def copy_for_each(x, axis):
    copies = jnp.broadcast_to(x, (lax.axis_size(axis), *x.shape))
    return lax.all_to_all(copies, axis, split_axis=0, concat_axis=0, tiled=True)


def joined_along(parts, dim):
    parts = jnp.moveaxis(parts, 0, dim)
    dims = parts.shape
    return parts.reshape(*dims[:dim], dims[dim] * dims[dim + 1], *dims[dim + 2 :])


def gather_directly(x, axis, dim):
    parts = copy_for_each(x, axis)
    return joined_along(parts, dim)


def cut_along(x, dim, size):
    before, after = (x.shape[:dim], x.shape[dim + 1 :])
    return jnp.moveaxis(x.reshape(*before, size, -1, *after), dim, 0)


def summed_on_arrival(x, axis, dim):
    size = lax.axis_size(axis)
    parts = lax.all_to_all(cut_along(x, dim, size), axis, 0, 0, tiled=True)
    return jnp.sum(parts, axis=0)


def total_of(x, axes):
    lines = x.reshape(-1)
    padded = filled_up(lines, lax.axis_size(axes))
    whole = gather_directly(summed_on_arrival(padded, axes, 0), axes, 0)
    return lax.slice_in_dim(whole, 0, len(lines)).reshape(x.shape)


def of_everyone(x, axis):
    everything = copy_for_each(x, axis)
    return jnp.sum(everything, axis=0)


def by_axis(x, axes):
    for axis in axes:
        x = lax.psum(x, axis)
    return x


def shrink(values):
    return jnp.sign(values) * jnp.maximum(jnp.abs(values) - threshold, 0.0)


def conjugate_solve(hessian, gradient):
    delta = jnp.zeros_like(gradient)
    residual = gradient
    direction = gradient
    power = jnp.sum(residual * residual, axis=1)
    for cg_step in range(CG_STEPS):
        image = jnp.einsum("bkl,bl->bk", hessian, direction, precision=lax.Precision.HIGHEST)
        alpha = power / jnp.sum(direction * image, axis=1)
        delta = delta + alpha[:, None] * direction
        residual = residual - alpha[:, None] * image
        power_next = jnp.sum(residual * residual, axis=1)
        direction = residual + (power_next / power)[:, None] * direction
        power = power_next
    return delta


def local(local_x, dual_var, consensus_old, blocks_data, row_index, labels):
    iterate = local_x[0]
    dual_local = dual_var[0]
    block_rows = blocks_data[0]
    index_rows = row_index[0]
    targets = labels[0].astype(jnp.float32)
    samples = targets.shape[0]
    target = consensus_old - dual_local
    flat_index = index_rows.reshape(-1)
    identity = jnp.eye(iterate.shape[1], dtype=jnp.float32)
    for newton_step in range(NEWTON_STEPS):
        rounded = iterate.astype(jnp.bfloat16)
        partial_value = jnp.einsum(
            "brk,bk->br", block_rows, rounded, preferred_element_type=jnp.float32
        )
        local_margins = jax.ops.segment_sum(
            partial_value.reshape(-1), flat_index, num_segments=samples
        )
        margins = total_of(local_margins, FEAT)
        prob = jax.nn.sigmoid(margins)
        misfit = prob - targets
        weights = prob * (1.0 - prob)
        misfit_rows = misfit[index_rows].astype(jnp.bfloat16)
        gradient = jnp.einsum(
            "brk,br->bk", block_rows, misfit_rows, preferred_element_type=jnp.float32
        )
        gradient = gradient + penalty * (iterate - target)
        weighted = (block_rows * weights[index_rows][:, :, None]).astype(jnp.bfloat16)
        hessian = (
            jnp.einsum("brk,brl->bkl", block_rows, weighted, preferred_element_type=jnp.float32)
            + penalty * identity
        )
        delta = conjugate_solve(hessian, gradient)
        iterate = iterate - damping * delta
    shards = lax.axis_size(("row", "col"))
    combined = iterate + dual_local
    totals = of_everyone(combined, ("row", "col"))
    consensus = shrink(totals / jnp.float32(shards))
    dual_next = dual_local + iterate - consensus
    primal_local = jnp.sum((iterate - consensus) ** 2)
    change_local = jnp.sum((consensus - consensus_old) ** 2)
    primal_total, change_total = (
        by_axis(primal_local, FEAT_ROW_COL),
        by_axis(change_local / jnp.float32(shards), FEAT_ROW_COL),
    )
    norms = jnp.stack(
        [jnp.sqrt(primal_total), penalty * jnp.sqrt(jnp.float32(shards) * change_total)]
    )
    return (iterate[None], dual_next[None], consensus, norms)


def solution(mesh):
    torus = Mesh(
        mesh.devices.reshape(8, 4, 2, mesh.shape["row"], mesh.shape["col"]),
        ("feat_0", "feat_1", "feat_2", "row", "col"),
    )
    placed = (
        P(("row", "col"), FEAT, None),
        P(("row", "col"), FEAT, None),
        P(FEAT, None),
        P(("row", "col"), FEAT, None, None),
        P(("row", "col"), FEAT, None),
        P(("row", "col"), None),
    )
    return jax.shard_map(
        local,
        mesh=torus,
        in_specs=placed,
        out_specs=(
            P(("row", "col"), FEAT, None),
            P(("row", "col"), FEAT, None),
            P(FEAT, None),
            P(),
        ),
        check_vma=False,
    )
```

profile of v0, /device:TPU:1, one launch (start us, length us, event | category | flops | bytes accessed | tf_op | source)
XLA Modules:
  0.0 213.6 jit_solution(8987383086924766513)
XLA Ops:
  0.7 0.7 fusion.68
  1.4 1.6 fusion.26
  3.0 11.8 %scatter_custom_fusion = f32[16384]{0:T(1024)} fusion(s32[2048]{0:T(1024)S(1)} %bitcast.161, f32[2048]{0:T(1024)S(1)} %bitcast.163, f32[]{:T(128)} %constant.9.clone.1), kind=kCustom, calls=%fused_computation.44 | custom fusion | flops 2048 | bytes 65540 | tf_op jit(solution)/shard_map/scatter-add | solution.py:101
  14.8 15.1 %all-to-all-start = ((f32[64,1,256]{2,1,0:T(1,128)}), f32[64,1,256]{2,1,0:T(1,128)S(1)}, u32[]{:S(2)}, u32[]{:S(2)}) async-start(f32[64,1,256]{2,1,0:T(1,128)} %bitcast.4), calls=%async_computation | async-start | bytes 131072 | tf_op jit(solution)/shard_map/all_to_all | solution.py:44
  30.0 11.0 %all-to-all-done = f32[64,1,256]{2,1,0:T(1,128)S(1)} async-done(((f32[64,1,256]{2,1,0:T(1,128)}), f32[64,1,256]{2,1,0:T(1,128)S(1)}, u32[]{:S(2)}, u32[]{:S(2)}) %all-to-all-start) | async-done | bytes 65568 | tf_op jit(solution)/shard_map/all_to_all | solution.py:44
  41.8 4.6 %all-to-all-start.1 = ((f32[64,1,256]{2,1,0:T(1,128)}), f32[64,1,256]{2,1,0:T(1,128)S(1)}, u32[]{:S(2)}, u32[]{:S(2)}) async-start(f32[64,1,256]{2,1,0:T(1,128)} %broadcast_in_dim.10), calls=%async_computation.1 | async-start | bytes 131072 | tf_op jit(solution)/shard_map/all_to_all | solution.py:23
  46.5 10.9 %all-to-all-done.1 = f32[64,1,256]{2,1,0:T(1,128)S(1)} async-done(((f32[64,1,256]{2,1,0:T(1,128)}), f32[64,1,256]{2,1,0:T(1,128)S(1)}, u32[]{:S(2)}, u32[]{:S(2)}) %all-to-all-start.1) | async-done | bytes 65568 | tf_op jit(solution)/shard_map/all_to_all | solution.py:23
  57.5 11.8 %gather_fusion.1 = f32[2048]{0:T(1024)S(1)} fusion(f32[16384]{0:T(1024)S(1)} %subtract_multiply_fusion.1, s32[2048]{0:T(1024)S(1)} %broadcast_clamp_fusion), kind=kCustom, calls=%fused_computation.1 | custom fusion | bytes 24576 | tf_op jit(solution)/shard_map/gather | solution.py:113
  69.3 13.1 %gather_fusion = bf16[2048]{0:T(1024)(128)(2,1)S(1)} fusion(bf16[16384]{0:T(1024)(128)(2,1)S(1)} %sub.52, s32[2048]{0:T(1024)S(1)} %broadcast_clamp_fusion), kind=kCustom, calls=%fused_computation | custom fusion | bytes 16384 | tf_op jit(solution)/shard_map/gather | solution.py:108
  82.7 0.9 fusion.9
  84.7 0.7 fusion.63
  87.1 11.3 %scatter_custom_fusion.1 = f32[16384]{0:T(1024)S(1)} fusion(s32[2048]{0:T(1024)S(1)} %bitcast.162, f32[2048]{0:T(1024)S(1)} %bitcast.164, f32[]{:T(128)} %constant.9.clone.1), kind=kCustom, calls=%fused_computation.42 | custom fusion | flops 2048 | bytes 65540 | tf_op jit(solution)/shard_map/scatter-add | solution.py:101
  98.4 14.8 %all_to_all.35 = f32[64,1,256]{2,1,0:T(1,128)S(1)} all-to-all(f32[64,1,256]{2,1,0:T(1,128)S(1)} %bitcast.149), channel_id=1, replica_groups=mesh['feat_0'=8,'feat_1'=4,'feat_2'=2,'row'=2,'col'=2] {'feat_0','feat_1..., dimensions={0} | all-to-all | bytes 131072 | tf_op jit(solution)/shard_map/all_to_all | solution.py:44
  113.3 14.8 %all_to_all.36 = f32[64,1,256]{2,1,0:T(1,128)S(1)} all-to-all(f32[64,1,256]{2,1,0:T(1,128)S(1)} %broadcast_in_dim.11), channel_id=1, replica_groups=mesh['feat_0'=8,'feat_1'=4,'feat_2'=2,'row'=2,'col'=2] {'feat_0','feat_1..., dimensions={0} | all-to-all | bytes 131072 | tf_op jit(solution)/shard_map/all_to_all | solution.py:23
  128.2 13.1 %gather_fusion.2 = bf16[2048]{0:T(1024)(128)(2,1)S(1)} fusion(bf16[16384]{0:T(1024)(128)(2,1)S(1)} %sub.59, s32[2048]{0:T(1024)S(1)} %broadcast_clamp_fusion), kind=kCustom, calls=%fused_computation.2 | custom fusion | bytes 16384 | tf_op jit(solution)/shard_map/gather | solution.py:108
  141.3 11.8 %gather_fusion.3 = f32[2048]{0:T(1024)S(1)} fusion(f32[16384]{0:T(1024)S(1)} %subtract_multiply_fusion, s32[2048]{0:T(1024)S(1)} %broadcast_clamp_fusion), kind=kCustom, calls=%fused_computation.3 | custom fusion | bytes 24576 | tf_op jit(solution)/shard_map/gather | solution.py:113
  153.3 0.9 fusion.15
  157.3 11.1 %all_to_all.37 = f32[4,4,256]{2,1,0:T(4,128)S(1)} all-to-all(f32[4,4,256]{2,1,0:T(4,128)S(1)} %broadcast_in_dim.13), channel_id=1, replica_groups=mesh['feat_0'=8,'feat_1'=4,'feat_2'=2,'row'=2,'col'=2] {'row','col'}, dimensions={0} | all-to-all | bytes 32768 | tf_op jit(solution)/shard_map/all_to_all | solution.py:23
  168.5 0.7 multiply_reduce_fusion.1
  170.5 11.9 %all-reduce = (f32[]{:T(128)}, f32[]{:T(128)}) all-reduce(f32[]{:T(128)S(6)} %div.107, f32[]{:T(128)} %get-tuple-element.4), channel_id=1, replica_groups=mesh['feat_0'=8,'feat_1'=4,'feat_2'=2,'row'=2,'col'=2] {'feat_0'}, use_global_device_ids=true, to_apply=%region_24.25 | all-reduce | flops 2 | bytes 16 | tf_op jit(solution)/shard_map/psum | solution.py:62
  182.4 7.4 %all-reduce.1 = (f32[]{:T(128)}, f32[]{:T(128)}) all-reduce(f32[]{:T(128)} %get-tuple-element.10, f32[]{:T(128)} %get-tuple-element.11), channel_id=1, replica_groups=mesh['feat_0'=8,'feat_1'=4,'feat_2'=2,'row'=2,'col'=2] {'feat_1'}, use_global_device_ids=true, to_apply=%region_25.26 | all-reduce | flops 2 | bytes 16 | tf_op jit(solution)/shard_map/psum | solution.py:62
  189.8 5.9 %all-reduce.4 = (f32[]{:T(128)}, f32[]{:T(128)}) all-reduce(f32[]{:T(128)} %get-tuple-element.12, f32[]{:T(128)} %get-tuple-element.13), channel_id=1, replica_groups=mesh['feat_0'=8,'feat_1'=4,'feat_2'=2,'row'=2,'col'=2] {'feat_2'}, use_global_device_ids=true, to_apply=%region_26.27 | all-reduce | flops 2 | bytes 16 | tf_op jit(solution)/shard_map/psum | solution.py:62
  195.7 4.5 %all-reduce.3 = (f32[]{:T(128)}, f32[]{:T(128)}) all-reduce(f32[]{:T(128)} %get-tuple-element.18, f32[]{:T(128)} %get-tuple-element.19), channel_id=1, replica_groups=mesh['feat_0'=8,'feat_1'=4,'feat_2'=2,'row'=2,'col'=2] {'row'}, use_global_device_ids=true, to_apply=%region_27.28 | all-reduce | flops 2 | bytes 16 | tf_op jit(solution)/shard_map/psum | solution.py:62
  200.1 11.6 %all-reduce.2 = (f32[]{:T(128)}, f32[]{:T(128)}) all-reduce(f32[]{:T(128)} %get-tuple-element.16, f32[]{:T(128)} %get-tuple-element.17), channel_id=1, replica_groups=mesh['feat_0'=8,'feat_1'=4,'feat_2'=2,'row'=2,'col'=2] {'col'}, use_global_device_ids=true, to_apply=%region_28.29 | all-reduce | flops 2 | bytes 16 | tf_op jit(solution)/shard_map/psum | solution.py:62
  (82 shorter events, 8.6 us)
Async XLA Ops:
  0.6 2.4 %copy-start.5 = (s32[1,4,512]{2,1,0:T(4,128)S(1)}, s32[1,4,512]{2,1,0:T(4,128)}, u32[]{:S(2)}) copy-start(s32[1,4,512]{2,1,0:T(4,128)} %param.10) | copy-start | bytes 24580
  0.6 45.8 %copy-start.1 = (s32[1,16384]{1,0:T(1,128)S(1)}, s32[1,16384]{1,0:T(1,128)}, u32[]{:S(2)}) copy-start(s32[1,16384]{1,0:T(1,128)} %param.11) | copy-start | bytes 196612
  14.8 26.2 %all-to-all-start = ((f32[64,1,256]{2,1,0:T(1,128)}), f32[64,1,256]{2,1,0:T(1,128)S(1)}, u32[]{:S(2)}, u32[]{:S(2)}) async-start(f32[64,1,256]{2,1,0:T(1,128)} %bitcast.4), calls=%async_computation | async-start | bytes 131072 | tf_op jit(solution)/shard_map/all_to_all | solution.py:44
  41.8 15.6 %all-to-all-start.1 = ((f32[64,1,256]{2,1,0:T(1,128)}), f32[64,1,256]{2,1,0:T(1,128)S(1)}, u32[]{:S(2)}, u32[]{:S(2)}) async-start(f32[64,1,256]{2,1,0:T(1,128)} %broadcast_in_dim.10), calls=%async_computation.1 | async-start | bytes 131072 | tf_op jit(solution)/shard_map/all_to_all | solution.py:23
  69.3 13.1 %copy-start = (bf16[1,4,512,256]{3,2,1,0:T(8,128)(2,1)S(1)}, bf16[1,4,512,256]{3,2,1,0:T(8,128)(2,1)}, u32[]{:S(2)}) copy-start(bf16[1,4,512,256]{3,2,1,0:T(8,128)(2,1)} %param.9) | copy-start | bytes 3145732
  82.7 0.9 copy-start.2
  82.7 1.0 copy-start.3
  82.7 1.0 copy-start.4
  157.3 56.2 %copy-start.7 = (f32[4,256]{1,0:T(4,128)}, f32[4,256]{1,0:T(4,128)S(1)}, u32[]{:S(2)}) copy-start(f32[4,256]{1,0:T(4,128)S(1)} %get-tuple-element.22) | copy-start | bytes 12292
  169.2 44.4 %copy-start.6 = (f32[4,256]{1,0:T(4,128)}, f32[4,256]{1,0:T(4,128)S(1)}, u32[]{:S(2)}) copy-start(f32[4,256]{1,0:T(4,128)S(1)} %get-tuple-element.20) | copy-start | bytes 12292
where the time goes:
time: 214 us
  blocking collectives  81.9 us (38%)
  local copies, waits for them, and re-layouts  50.6 us (24%)
  other arithmetic  28.1 us (13%)
  waiting for transfers between devices  21.9 us (10%)
  starting transfers between devices  19.7 us (9%)
  matrix products  8.28 us (4%)
  between operations  3 us (1%)
    psum x5, blocking collectives, by_axis(): x = lax.psum(x, axis)  41.2 us
    gather x2, local copies, waits for them, and re-layouts, local(): misfit_rows = misfit[index_rows].astype(jnp.bfloat16)  26.2 us
    all_to_all x2, blocking collectives, copy_for_each(): return lax.all_to_all(copies, axis, split_axis=0, concat_axis=0, tiled=True)  25.9 us
    gather x4, local copies, waits for them, and re-layouts, local(): weights[index_rows][:, :, None]  23.6 us
    scatter-add x2, other arithmetic, local(): jax.ops.segment_sum(partial_value.reshape(-1), flat_index, num_segments=s...  23.1 us
    all_to_all x1, starting transfers between devices, summed_on_arrival(): parts = lax.all_to_all(cut_along(x, dim, size), axis, 0, 0, tiled=True)  15.1 us
    all_to_all x1, blocking collectives, summed_on_arrival(): parts = lax.all_to_all(cut_along(x, dim, size), axis, 0, 0, tiled=True)  14.8 us
    all_to_all x1, waiting for transfers between devices, summed_on_arrival(): parts = lax.all_to_all(cut_along(x, dim, size), axis, 0, 0, tiled=True)  11 us
  transfers between devices with their start and end apart: 2, of which 2 were waited for; matrix products, arithmetic and copies ran while one was open for 0% of the time, Pallas kernels for 0%

commit v1 on v0

--- a/solution.py
+++ b/solution.py
@@ -59,7 +59,7 @@
 
 def by_axis(x, axes):
     for axis in axes:
-        x = lax.psum(x, axis)
+        x = jnp.sum(lax.all_gather(x, axis), axis=0)
     return x
 
 

time: 214 us -> 235 us (1.098)
  local copies, waits for them, and re-layouts: 50.6 us -> 68.3 us
  blocking collectives: 81.9 us -> 67.4 us
  starting transfers between devices: 19.7 us -> 28.6 us
  other arithmetic: 28.1 us -> 34.4 us
  waiting for transfers between devices: 21.9 us -> 24.5 us
    psum x5 -> x0, blocking collectives: 41.2 us -> none  [by_axis(): x = lax.psum(x, axis)]
    unnamed x0 -> x5, blocking collectives: none -> 37.8 us
    unnamed x22 -> x57, local copies, waits for them, and re-layouts: 0.13 us -> 17.2 us
    all_to_all x2 -> x1, blocking collectives: 25.9 us -> 14.8 us  [copy_for_each(): return lax.all_to_all(copies, axis, split_axis=0, concat_axis=0, tiled=True)]
    all_to_all x1 -> x2, starting transfers between devices: 4.61 us -> 13.5 us  [copy_for_each(): return lax.all_to_all(copies, axis, split_axis=0, concat_axis=0, tiled=True)]
    reduce_sum x0 -> x10, other arithmetic: none -> 6.33 us  [by_axis(): x = jnp.sum(lax.all_gather(x, axis), axis=0)]
    all_to_all x1 -> x2, waiting for transfers between devices: 10.9 us -> 13.4 us  [copy_for_each(): return lax.all_to_all(copies, axis, split_axis=0, concat_axis=0, tiled=True)]
  transfers between devices with their start and end apart: 2 -> 3, of which waited for: 2 -> 3; matrix products, arithmetic and copies ran while one was open for 0% -> 0% of each run, Pallas kernels for 0% -> 0%
where the time goes in v1:
time: 235 us; the launch traced here: 234 us
  local copies, waits for them, and re-layouts  68.3 us (29%)
  blocking collectives  67.4 us (29%)
  other arithmetic  34.4 us (15%)
  starting transfers between devices  28.6 us (12%)
  waiting for transfers between devices  24.5 us (10%)
  matrix products  8.26 us (4%)
  between operations  3.1 us (1%)
    unnamed x5, blocking collectives  37.8 us
    gather x2, local copies, waits for them, and re-layouts, local(): misfit_rows = misfit[index_rows].astype(jnp.bfloat16)  26.2 us
    gather x4, local copies, waits for them, and re-layouts, local(): weights[index_rows][:, :, None]  23.6 us
    scatter-add x2, other arithmetic, local(): jax.ops.segment_sum(partial_value.reshape(-1), flat_index, num_segments=s...  23.1 us
    unnamed x57, local copies, waits for them, and re-layouts  17.2 us
    all_to_all x1, starting transfers between devices, summed_on_arrival(): parts = lax.all_to_all(cut_along(x, dim, size), axis, 0, 0, tiled=True)  15.1 us
    all_to_all x1, blocking collectives, copy_for_each(): return lax.all_to_all(copies, axis, split_axis=0, concat_axis=0, tiled=True)  14.8 us
    all_to_all x1, blocking collectives, summed_on_arrival(): parts = lax.all_to_all(cut_along(x, dim, size), axis, 0, 0, tiled=True)  14.8 us
  transfers between devices with their start and end apart: 3, of which 3 were waited for; matrix products, arithmetic and copies ran while one was open for 0% of the time, Pallas kernels for 0%

profile of v1, /device:TPU:1, one launch (start us, length us, event | category | flops | bytes accessed | tf_op | source)
XLA Modules:
  0.0 234.5 jit_solution(4961738599127957706)
XLA Ops:
  2.1 1.6 fusion.26
  3.7 11.8 %scatter_custom_fusion = f32[16384]{0:T(1024)} fusion(s32[2048]{0:T(1024)S(1)} %bitcast.176, f32[2048]{0:T(1024)S(1)} %bitcast.179, f32[]{:T(128)} %constant.9.clone.1), kind=kCustom, calls=%fused_computation.44 | custom fusion | flops 2048 | bytes 65540 | tf_op jit(solution)/shard_map/scatter-add | solution.py:101
  15.5 15.1 %all-to-all-start = ((f32[64,1,256]{2,1,0:T(1,128)}), f32[64,1,256]{2,1,0:T(1,128)S(1)}, u32[]{:S(2)}, u32[]{:S(2)}) async-start(f32[64,1,256]{2,1,0:T(1,128)} %bitcast.4), calls=%async_computation | async-start | bytes 131072 | tf_op jit(solution)/shard_map/all_to_all | solution.py:44
  30.7 11.0 %all-to-all-done = f32[64,1,256]{2,1,0:T(1,128)S(1)} async-done(((f32[64,1,256]{2,1,0:T(1,128)}), f32[64,1,256]{2,1,0:T(1,128)S(1)}, u32[]{:S(2)}, u32[]{:S(2)}) %all-to-all-start) | async-done | bytes 65568 | tf_op jit(solution)/shard_map/all_to_all | solution.py:44
  42.5 4.6 %all-to-all-start.1 = ((f32[64,1,256]{2,1,0:T(1,128)}), f32[64,1,256]{2,1,0:T(1,128)S(1)}, u32[]{:S(2)}, u32[]{:S(2)}) async-start(f32[64,1,256]{2,1,0:T(1,128)} %broadcast_in_dim.10), calls=%async_computation.1 | async-start | bytes 131072 | tf_op jit(solution)/shard_map/all_to_all | solution.py:23
  47.2 10.9 %all-to-all-done.1 = f32[64,1,256]{2,1,0:T(1,128)S(1)} async-done(((f32[64,1,256]{2,1,0:T(1,128)}), f32[64,1,256]{2,1,0:T(1,128)S(1)}, u32[]{:S(2)}, u32[]{:S(2)}) %all-to-all-start.1) | async-done | bytes 65568 | tf_op jit(solution)/shard_map/all_to_all | solution.py:23
  58.2 13.1 %gather_fusion = bf16[2048]{0:T(1024)(128)(2,1)S(1)} fusion(bf16[16384]{0:T(1024)(128)(2,1)S(1)} %sub.52, s32[2048]{0:T(1024)S(1)} %broadcast_clamp_fusion), kind=kCustom, calls=%fused_computation | custom fusion | bytes 16384 | tf_op jit(solution)/shard_map/gather | solution.py:108
  71.6 11.8 %gather_fusion.1 = f32[2048]{0:T(1024)S(1)} fusion(f32[16384]{0:T(1024)S(1)} %subtract_multiply_fusion.1, s32[2048]{0:T(1024)S(1)} %broadcast_clamp_fusion), kind=kCustom, calls=%fused_computation.1 | custom fusion | bytes 24576 | tf_op jit(solution)/shard_map/gather | solution.py:113
  87.8 11.3 %scatter_custom_fusion.1 = f32[16384]{0:T(1024)S(1)} fusion(s32[2048]{0:T(1024)S(1)} %bitcast.177, f32[2048]{0:T(1024)S(1)} %bitcast.178, f32[]{:T(128)} %constant.9.clone.1), kind=kCustom, calls=%fused_computation.42 | custom fusion | flops 2048 | bytes 65540 | tf_op jit(solution)/shard_map/scatter-add | solution.py:101
  99.1 14.8 %all_to_all.36 = f32[64,1,256]{2,1,0:T(1,128)S(1)} all-to-all(f32[64,1,256]{2,1,0:T(1,128)S(1)} %bitcast.164), channel_id=1, replica_groups=mesh['feat_0'=8,'feat_1'=4,'feat_2'=2,'row'=2,'col'=2] {'feat_0','feat_1..., dimensions={0} | all-to-all | bytes 131072 | tf_op jit(solution)/shard_map/all_to_all | solution.py:44
  114.0 14.8 %all_to_all.35 = f32[64,1,256]{2,1,0:T(1,128)S(1)} all-to-all(f32[64,1,256]{2,1,0:T(1,128)S(1)} %broadcast_in_dim.11), channel_id=1, replica_groups=mesh['feat_0'=8,'feat_1'=4,'feat_2'=2,'row'=2,'col'=2] {'feat_0','feat_1..., dimensions={0} | all-to-all | bytes 131072 | tf_op jit(solution)/shard_map/all_to_all | solution.py:23
  128.9 13.1 %gather_fusion.2 = bf16[2048]{0:T(1024)(128)(2,1)S(1)} fusion(bf16[16384]{0:T(1024)(128)(2,1)S(1)} %sub.59, s32[2048]{0:T(1024)S(1)} %broadcast_clamp_fusion), kind=kCustom, calls=%fused_computation.2 | custom fusion | bytes 16384 | tf_op jit(solution)/shard_map/gather | solution.py:108
  142.3 11.8 %gather_fusion.3 = f32[2048]{0:T(1024)S(1)} fusion(f32[16384]{0:T(1024)S(1)} %subtract_multiply_fusion, s32[2048]{0:T(1024)S(1)} %broadcast_clamp_fusion), kind=kCustom, calls=%fused_computation.3 | custom fusion | bytes 24576 | tf_op jit(solution)/shard_map/gather | solution.py:113
  158.7 8.9 %all-to-all-start.4 = ((f32[4,4,256]{2,1,0:T(4,128)}), f32[4,4,256]{2,1,0:T(4,128)S(1)}, u32[]{:S(2)}, u32[]{:S(2)}) async-start(f32[4,4,256]{2,1,0:T(4,128)} %broadcast_in_dim.13), calls=%async_computation.4 | async-start | bytes 32768 | tf_op jit(solution)/shard_map/all_to_all | solution.py:23
  168.1 2.6 %all-to-all-done.4 = f32[4,4,256]{2,1,0:T(4,128)S(1)} async-done(((f32[4,4,256]{2,1,0:T(4,128)}), f32[4,4,256]{2,1,0:T(4,128)S(1)}, u32[]{:S(2)}, u32[]{:S(2)}) %all-to-all-start.4) | async-done | bytes 16416 | tf_op jit(solution)/shard_map/all_to_all | solution.py:23
  174.5 11.2 %all-reduce.10 = (f32[8]{0:T(128)S(1)}, f32[8]{0:T(128)S(1)}) all-reduce(f32[8]{0:T(128)S(1)} %dynamic-update-slice.5, f32[8]{0:T(128)S(1)} %dynamic-update-slice), channel_id=1, replica_groups=mesh['feat_0'=8,'feat_1'=4,'feat_2'=2,'row'=2,'col'=2] {'feat_0'}, use_global_device_ids=true, to_apply=%add.5 | all-reduce | flops 16 | bytes 128
  188.5 1.4 dynamic-update-slice.1
  190.5 6.7 %all-reduce.11 = (f32[4]{0:T(128)S(1)}, f32[4]{0:T(128)S(1)}) all-reduce(f32[4]{0:T(128)S(1)} %dynamic-update-slice.6, f32[4]{0:T(128)S(1)} %dynamic-update-slice.1), channel_id=1, replica_groups=mesh['feat_0'=8,'feat_1'=4,'feat_2'=2,'row'=2,'col'=2] {'feat_1'}, use_global_device_ids=true, to_apply=%add.6 | all-reduce | flops 8 | bytes 64
  199.9 1.4 dynamic-update-slice.2
  201.9 5.3 %all-reduce.14 = (f32[2]{0:T(128)S(1)}, f32[2]{0:T(128)S(1)}) all-reduce(f32[2]{0:T(128)S(1)} %dynamic-update-slice.7, f32[2]{0:T(128)S(1)} %dynamic-update-slice.2), channel_id=1, replica_groups=mesh['feat_0'=8,'feat_1'=4,'feat_2'=2,'row'=2,'col'=2] {'feat_2'}, use_global_device_ids=true, to_apply=%add.7 | all-reduce | flops 4 | bytes 32
  209.8 1.4 dynamic-update-slice.3
  211.9 3.8 %all-reduce.13 = (f32[2]{0:T(128)S(1)}, f32[2]{0:T(128)S(1)}) all-reduce(f32[2]{0:T(128)S(1)} %dynamic-update-slice.8, f32[2]{0:T(128)S(1)} %dynamic-update-slice.3), channel_id=1, replica_groups=mesh['feat_0'=8,'feat_1'=4,'feat_2'=2,'row'=2,'col'=2] {'row'}, use_global_device_ids=true, to_apply=%add.8 | all-reduce | flops 4 | bytes 32
  218.3 1.4 dynamic-update-slice.4
  220.4 10.9 %all-reduce.12 = (f32[2]{0:T(128)S(1)}, f32[2]{0:T(128)S(1)}) all-reduce(f32[2]{0:T(128)S(1)} %dynamic-update-slice.9, f32[2]{0:T(128)S(1)} %dynamic-update-slice.4), channel_id=1, replica_groups=mesh['feat_0'=8,'feat_1'=4,'feat_2'=2,'row'=2,'col'=2] {'col'}, use_global_device_ids=true, to_apply=%add.9 | all-reduce | flops 4 | bytes 32
  (128 shorter events, 30.7 us)
Async XLA Ops:
  0.6 30.0 %copy-start.5 = (s32[1,4,512]{2,1,0:T(4,128)S(1)}, s32[1,4,512]{2,1,0:T(4,128)}, u32[]{:S(2)}) copy-start(s32[1,4,512]{2,1,0:T(4,128)} %param.10) | copy-start | bytes 24580
  0.6 46.5 %copy-start.1 = (s32[1,16384]{1,0:T(1,128)S(1)}, s32[1,16384]{1,0:T(1,128)}, u32[]{:S(2)}) copy-start(s32[1,16384]{1,0:T(1,128)} %param.11) | copy-start | bytes 196612
  15.5 26.2 %all-to-all-start = ((f32[64,1,256]{2,1,0:T(1,128)}), f32[64,1,256]{2,1,0:T(1,128)S(1)}, u32[]{:S(2)}, u32[]{:S(2)}) async-start(f32[64,1,256]{2,1,0:T(1,128)} %bitcast.4), calls=%async_computation | async-start | bytes 131072 | tf_op jit(solution)/shard_map/all_to_all | solution.py:44
  42.5 15.6 %all-to-all-start.1 = ((f32[64,1,256]{2,1,0:T(1,128)}), f32[64,1,256]{2,1,0:T(1,128)S(1)}, u32[]{:S(2)}, u32[]{:S(2)}) async-start(f32[64,1,256]{2,1,0:T(1,128)} %broadcast_in_dim.10), calls=%async_computation.1 | async-start | bytes 131072 | tf_op jit(solution)/shard_map/all_to_all | solution.py:23
  58.2 13.1 %copy-start = (bf16[1,4,512,256]{3,2,1,0:T(8,128)(2,1)S(1)}, bf16[1,4,512,256]{3,2,1,0:T(8,128)(2,1)}, u32[]{:S(2)}) copy-start(bf16[1,4,512,256]{3,2,1,0:T(8,128)(2,1)} %param.9) | copy-start | bytes 3145732
  83.4 1.0 copy-start.2
  83.4 1.0 copy-start.3
  83.4 1.0 copy-start.4
  156.1 11.4 %copy-start.12 = (u32[256]{0:T(256)S(1)}, u32[256]{0:T(256)}, u32[]{:S(2)}) copy-start(u32[256]{0:T(256)} %constant.30) | copy-start | bytes 3076
  156.1 17.8 %copy-start.11 = (u32[256]{0:T(256)S(1)}, u32[256]{0:T(256)}, u32[]{:S(2)}) copy-start(u32[256]{0:T(256)} %constant.35) | copy-start | bytes 3076
  156.1 33.8 %copy-start.10 = (u32[256]{0:T(256)S(1)}, u32[256]{0:T(256)}, u32[]{:S(2)}) copy-start(u32[256]{0:T(256)} %constant.40) | copy-start | bytes 3076
  156.1 45.2 %copy-start.9 = (u32[256]{0:T(256)S(1)}, u32[256]{0:T(256)}, u32[]{:S(2)}) copy-start(u32[256]{0:T(256)} %constant.45) | copy-start | bytes 3076
  156.1 55.2 %copy-start.8 = (u32[256]{0:T(256)S(1)}, u32[256]{0:T(256)}, u32[]{:S(2)}) copy-start(u32[256]{0:T(256)} %constant.50) | copy-start | bytes 3076
  158.1 76.4 %copy-start.7 = (f32[4,256]{1,0:T(4,128)}, f32[4,256]{1,0:T(4,128)S(1)}, u32[]{:S(2)}) copy-start(f32[4,256]{1,0:T(4,128)S(1)} %get-tuple-element.22) | copy-start | bytes 12292
  158.7 12.0 %all-to-all-start.4 = ((f32[4,4,256]{2,1,0:T(4,128)}), f32[4,4,256]{2,1,0:T(4,128)S(1)}, u32[]{:S(2)}, u32[]{:S(2)}) async-start(f32[4,4,256]{2,1,0:T(4,128)} %broadcast_in_dim.13), calls=%async_computation.4 | async-start | bytes 32768 | tf_op jit(solution)/shard_map/all_to_all | solution.py:23
  171.3 63.2 %copy-start.6 = (f32[4,256]{1,0:T(4,128)}, f32[4,256]{1,0:T(4,128)S(1)}, u32[]{:S(2)}) copy-start(f32[4,256]{1,0:T(4,128)S(1)} %get-tuple-element.20) | copy-start | bytes 12292
